TPU v7x, 256 devices: a whole 4x4x8 slice. The times are simulated.
256 devices in a mesh: seq: 32 (over y, x, core), vocab: 8 (over z).
Axes of the slice: x: 4, y: 4, z: 8, core: 2. Of those that a mesh axis runs over, the one named last changes fastest.
Arguments:
- hidden: bfloat16 [4096, 8192], P('seq'), may hold values from -120 to 120
- head: bfloat16 [8192, 65536], P(None, ('seq', 'vocab')), may hold values from -0.5 to 0.5
- mask: int32 [4096], P('seq'), may hold values from 0 to 1, as said below
Outputs:
- positionwise_uncertainty: float32 [4096], P('seq')
- average_uncertainty_reward: float32 [], replicated
- derivative_wrt_latent_vectors: bfloat16 [4096, 8192], P('seq', 'vocab')
Inputs may be any that keep to these rules, and one draw needn't show every extreme that they name: Among the 128 tokens of one index of seq at least half of 16 and at most 16 have mask 1, and the last index of seq has exactly 16; later indices have no fewer than earlier ones.
All inputs are finite; a program needn't handle non-finite values.
Results may differ from a plain program's by a relative error of at most 0.019.
Values may be sent and summed in bfloat16 or wider, within the bound.
A program may use at most 64 MiB of HBM per device.

v0:
```python
import jax
import jax.numpy as jnp
from jax import lax
from jax.sharding import Mesh
from jax.sharding import PartitionSpec as P

ACT_DEV = 16
SEQ = ("seq_0", "seq_1", "seq_2")
SEQ_VOCAB = ("seq_0", "seq_1", "seq_2", "vocab")


def gathered_once(array, axis):
    leaves = jax.tree.leaves(array)
    sequence = sorted(range(len(leaves)), key=lambda k: -leaves[k].size)
    width = (1, *leaves[sequence[0]].shape)[-1]
    lines = [
        jnp.pad(leaves[k].reshape(-1), (0, -leaves[k].size % width)).reshape(-1, width)
        for k in sequence
    ]
    both, at, found = (lax.all_gather(jnp.concatenate(lines), axis), 0, {})
    for k, line in zip(sequence, lines):
        slab = both[:, at : at + len(line)].reshape(len(both), -1)
        found[k] = slab[:, : leaves[k].size].reshape(-1, *leaves[k].shape)
        at += len(line)
    numbers = iter(range(len(leaves)))
    return jax.tree.map(lambda _: found[next(numbers)], array)


def combined_by_axis(array, axes, combine):
    for axis in axes:
        pieces = gathered_once(array, axis)
        array = jax.tree.map(lambda part: part[0], pieces)
        for k in range(1, lax.axis_size(axis)):
            array = combine(array, jax.tree.map(lambda part: part[k], pieces))
    return array


def cut_along(array, dim, devices):
    before, after = (array.shape[:dim], array.shape[dim + 1 :])
    return jnp.moveaxis(array.reshape(*before, devices, -1, *after), dim, 0)


def sent_and_summed(array, axis, dim):
    pieces = cut_along(array, dim, lax.axis_size(axis))
    arrived = lax.all_to_all(pieces, axis, split_axis=0, concat_axis=0, tiled=True)
    return arrived.astype(jnp.float32).sum(axis=0)


def from_everyone(array, axis):
    devices = lax.axis_size(axis)
    return lax.all_to_all(
        jnp.broadcast_to(array[None], (devices, *array.shape)), axis, 0, 0, tiled=True
    )


def taken_together(array, axis):
    return from_everyone(array, axis).sum(axis=0)


def packed_total(arrays, axis):
    ends = [0]
    for a in arrays:
        ends.append(ends[-1] + a.size)
    total = taken_together(jnp.concatenate([a.ravel() for a in arrays]), axis)
    return tuple((total[b:e].reshape(a.shape) for a, b, e in zip(arrays, ends, ends[1:])))


def combine_rows(first, second):
    top = jnp.maximum(first[0], second[0])
    left = jnp.exp(first[0] - top)
    right = jnp.exp(second[0] - top)
    return (top, first[1] * left + second[1] * right, first[2] * left + second[2] * right)


def body(hidden, head, mask):
    inclusion_indicator = mask.astype(jnp.float32)
    slots = jnp.cumsum(mask) - 1
    picker = (slots[None, :] == jnp.arange(ACT_DEV, dtype=jnp.int32)[:, None]) & (
        mask[None, :] == 1
    )
    picker = picker.astype(jnp.bfloat16)
    source = jnp.dot(picker, hidden, preferred_element_type=jnp.float32).astype(jnp.bfloat16)
    rows_here = source.shape[0]
    logits = jnp.dot(
        lax.all_gather(source, SEQ, axis=0, tiled=True), head, preferred_element_type=jnp.float32
    )
    local_top = jnp.max(logits, axis=1)
    local_ex = jnp.exp(logits - local_top[:, None])
    top, total, weighted = combined_by_axis(
        (local_top, jnp.sum(local_ex, axis=1), jnp.sum(local_ex * logits, axis=1)),
        SEQ_VOCAB,
        combine_rows,
    )
    ex = jnp.exp(logits - top[:, None])
    mean_logit = weighted / total
    distribution_uncertainty = top + jnp.log(total) - mean_logit
    prob = ex / total[:, None]
    score_grad = (-(prob * (logits - mean_logit[:, None]))).astype(jnp.bfloat16)
    partial_grad = lax.psum_scatter(
        lax.dot_general(
            score_grad, head, (((1,), (1,)), ((), ())), preferred_element_type=jnp.float32
        ).astype(jnp.bfloat16),
        SEQ,
        scatter_dimension=0,
        tiled=True,
    )
    column_grad = sent_and_summed(partial_grad, "vocab", 1)
    position = lax.axis_index(SEQ) * rows_here
    mine = lax.dynamic_slice_in_dim(distribution_uncertainty, position, rows_here, 0)
    spread = picker.astype(jnp.float32)
    mine = lax.dot_general(
        spread, mine[:, None], (((0,), (0,)), ((), ())), precision=lax.Precision.HIGHEST
    )[:, 0]
    column_grad = lax.dot_general(
        spread, column_grad, (((0,), (0,)), ((), ())), precision=lax.Precision.HIGHEST
    )
    positionwise_uncertainty = inclusion_indicator * mine
    aggregate_uncertainty, response_length_total = packed_total(
        (jnp.sum(positionwise_uncertainty), jnp.sum(inclusion_indicator)), SEQ
    )
    average_uncertainty_reward = aggregate_uncertainty / response_length_total
    derivative_wrt_latent_vectors = (inclusion_indicator[:, None] * column_grad).astype(
        jnp.bfloat16
    )
    return (positionwise_uncertainty, average_uncertainty_reward, derivative_wrt_latent_vectors)


def solution(mesh):
    finer = Mesh(
        mesh.devices.reshape(4, 4, 2, mesh.shape["vocab"]), ("seq_0", "seq_1", "seq_2", "vocab")
    )
    placed = (P(SEQ, None), P(None, SEQ_VOCAB), P(SEQ))
    return jax.shard_map(
        body, mesh=finer, in_specs=placed, out_specs=(P(SEQ), P(), P(SEQ, "vocab")), check_vma=False
    )
```

profile of v0, /device:TPU:2, one launch (start us, length us, event | category | flops | bytes accessed | tf_op | source)
XLA Modules:
  0.0 263.5 jit_solution(15623832513023680919)
XLA Ops:
  7.2 0.0 copy-start
  7.2 0.0 all-gather.10.cloned.1.call-start
  7.2 0.8 broadcast_compare_fusion
  8.0 0.8 copy.12
  8.8 0.2 reduce-window.8
  9.0 0.1 add_reduce_fusion
  9.1 1.1 convolution_convert_fusion.1
  10.2 0.0 all-gather.10.cloned.1.call-update
  10.2 0.0 reduce-scatter.2.cloned.1.call-start
  10.2 61.6 %all-gather.10.cloned.1.call-done = bf16[512,8192]{1,0:T(8,128)(2,1)} async-done(((bf16[16,8192]{1,0:T(8,128)(2,1)}), bf16[512,8192]{1,0:T(8,128)(2,1)}) %all-gather.10.cloned.1.call-update) | async-done | bytes 8388624 | tf_op jit(solution)/shard_map/all_gather | solution.py:85
  71.9 7.1 %fusion.72 = (f32[512]{0:T(512)S(1)}, f32[512,256]{0,1:T(8,128)S(1)}) fusion(bf16[512,8192]{1,0:T(8,128)(2,1)} %all-gather.10.cloned.1.call-done, bf16[8192,256]{1,0:T(8,128)(2,1)} %param.4), kind=kOutput, calls=%fused_computation.146 | convolution fusion | flops 2147614208 | bytes 13109248 | tf_op jit(solution)/shard_map/dot_general | solution.py:84
  79.0 0.1 fusion.2
  79.2 11.9 %all-gather.4 = f32[4,3,512]{2,1,0:T(4,128)S(1)} all-gather(f32[1,3,512]{2,1,0:T(4,128)S(1)} %maximum_bitcast_fusion), channel_id=2, replica_groups=mesh['seq_0'=4,'seq_1'=4,'seq_2'=2,'vocab'=8] {'seq_0'}, dimensions={0}, use_global_device_ids=true | all-gather | bytes 30720 | tf_op jit(solution)/shard_map/all_gather | solution.py:20
  91.2 11.9 %all-gather.5 = f32[4,3,512]{2,1,0:T(4,128)S(1)} all-gather(f32[1,3,512]{2,1,0:T(4,128)S(1)} %maximum_bitcast_fusion.1), channel_id=3, replica_groups=mesh['seq_0'=4,'seq_1'=4,'seq_2'=2,'vocab'=8] {'seq_1'}, dimensions={0}, use_global_device_ids=true | all-gather | bytes 30720 | tf_op jit(solution)/shard_map/all_gather | solution.py:20
  103.2 1.8 all-gather.6
  105.1 26.0 %all-gather.7 = f32[8,3,512]{2,1,0:T(4,128)S(1)} all-gather(f32[1,3,512]{2,1,0:T(4,128)S(1)} %maximum_bitcast_fusion.3), channel_id=5, replica_groups=mesh['seq_0'=4,'seq_1'=4,'seq_2'=2,'vocab'=8] {'vocab'}, dimensions={0}, use_global_device_ids=true | all-gather | bytes 55296 | tf_op jit(solution)/shard_map/all_gather | solution.py:20
  131.2 0.1 add_subtract_fusion
  131.3 5.6 %convolution_convert_fusion = bf16[512,8192]{1,0:T(8,128)(2,1)} fusion(bf16[8192,256]{1,0:T(8,128)(2,1)S(1)} %copy-done.1, f32[512,256]{0,1:T(8,128)S(1)} %get-tuple-element.48, f32[512]{0:T(512)S(1)} %get-tuple-element.6, f32[512]{0:T(512)S(1)} %get-tuple-element.7, f32[512]{0:T(512)S(1)} %get-tuple-element.8), kind=kOutput, calls=%fused_computation | convolution fusion | flops 2152464384 | bytes 13113344 | tf_op jit(solution)/shard_map/dot_general | solution.py:100
  136.9 0.0 reduce-scatter.2.cloned.1.call-update
  136.9 0.6 copy-done.2
  137.6 0.6 convert_reduce_fusion.1
  138.2 1.3 fusion.73
  139.5 1.4 pad_maximum_fusion
  140.8 0.6 broadcast_in_dim.2
  141.4 5.6 %all-to-all-start = ((f32[32,1,2]{2,1,0:T(1,128)}), f32[32,1,2]{2,1,0:T(1,128)S(1)}, u32[]{:S(2)}, u32[]{:S(2)}) async-start(f32[32,1,2]{2,1,0:T(1,128)} %broadcast_in_dim.2), calls=%async_computation | async-start | bytes 32768 | tf_op jit(solution)/shard_map/all_to_all | solution.py:51
  147.0 88.1 %reduce-scatter.2.cloned.1.call-done = bf16[16,8192]{1,0:T(8,128)(2,1)} async-done(((bf16[512,8192]{1,0:T(8,128)(2,1)}), bf16[16,8192]{1,0:T(8,128)(2,1)}) %reduce-scatter.2.cloned.1.call-update) | async-done | bytes 262160 | tf_op jit(solution)/shard_map/reduce_scatter | solution.py:99
  235.2 1.7 copy.20
  236.8 7.0 %all-to-all-start.1 = ((bf16[8,16,1024]{2,1,0:T(8,128)(2,1)}), bf16[8,16,1024]{2,1,0:T(8,128)(2,1)S(1)}, u32[]{:S(2)}, u32[]{:S(2)}) async-start(bf16[8,16,1024]{2,1,0:T(8,128)(2,1)} %bitcast.357), calls=%async_computation.2 | async-start | bytes 524288 | tf_op jit(solution)/shard_map/all_to_all | solution.py:45
  243.9 0.1 reduce_sum.58
  243.9 0.6 fusion.71
  245.9 8.4 %all-to-all-done.1 = bf16[8,16,1024]{2,1,0:T(8,128)(2,1)S(1)} async-done(((bf16[8,16,1024]{2,1,0:T(8,128)(2,1)}), bf16[8,16,1024]{2,1,0:T(8,128)(2,1)S(1)}, u32[]{:S(2)}, u32[]{:S(2)}) %all-to-all-start.1) | async-done | bytes 262176 | tf_op jit(solution)/shard_map/all_to_all | solution.py:45
  254.4 1.1 fusion
  (20 shorter events, 0.3 us)
Async XLA Ops:
  7.2 1.9 copy-start
  7.2 64.7 %all-gather.10.cloned.1.call-start = ((), (), s32[]{:S(2)}) async-start(), calls=%async_computation.3 | async-start | bytes 8650752 | tf_op jit(solution)/shard_map/all_gather | solution.py:85
  10.2 225.0 %reduce-scatter.2.cloned.1.call-start = ((), (), s32[]{:S(2)}) async-start(), calls=%async_computation.4 | async-start | bytes 8650752 | tf_op jit(solution)/shard_map/reduce_scatter | solution.py:99
  71.9 59.4 %copy-start.1 = (bf16[8192,256]{1,0:T(8,128)(2,1)S(1)}, bf16[8192,256]{1,0:T(8,128)(2,1)}, u32[]{:S(2)}) copy-start(bf16[8192,256]{1,0:T(8,128)(2,1)} %param.4) | copy-start | bytes 12582916
  136.9 0.7 copy-start.2
  141.4 95.4 %all-to-all-start = ((f32[32,1,2]{2,1,0:T(1,128)}), f32[32,1,2]{2,1,0:T(1,128)S(1)}, u32[]{:S(2)}, u32[]{:S(2)}) async-start(f32[32,1,2]{2,1,0:T(1,128)} %broadcast_in_dim.2), calls=%async_computation | async-start | bytes 32768 | tf_op jit(solution)/shard_map/all_to_all | solution.py:51
  236.8 17.5 %all-to-all-start.1 = ((bf16[8,16,1024]{2,1,0:T(8,128)(2,1)}), bf16[8,16,1024]{2,1,0:T(8,128)(2,1)S(1)}, u32[]{:S(2)}, u32[]{:S(2)}) async-start(bf16[8,16,1024]{2,1,0:T(8,128)(2,1)} %bitcast.357), calls=%async_computation.2 | async-start | bytes 524288 | tf_op jit(solution)/shard_map/all_to_all | solution.py:45
Sparse Core Ops, SparseCore 0:
  11.1 60.7 all-gather.9
  137.0 98.0 reduce-scatter.1
where the time goes:
time: 264 us; the launch traced here: 263 us
  waiting for transfers between devices  158 us (60%)
  blocking collectives  51.7 us (20%)
  between operations  16.7 us (6%)
  matrix products  16.3 us (6%)
  starting transfers between devices  12.7 us (5%)
  local copies, waits for them, and re-layouts  4.31 us (2%)
  other arithmetic  3.53 us (1%)
    reduce_scatter x1, waiting for transfers between devices, body(): lax.psum_scatter(lax.dot_general(score_grad, head, (((1,), (1,)), ((), ()...  88.1 us
    all_gather x1, waiting for transfers between devices, body(): lax.all_gather(source, SEQ, axis=0, tiled=True)  61.6 us
    all_gather x4, blocking collectives, gathered_once(): both, at, found = (lax.all_gather(jnp.concatenate(lines), axis), 0, {})  51.7 us
    all_to_all x1, waiting for transfers between devices, sent_and_summed(): lax.all_to_all(pieces, axis, split_axis=0, concat_axis=0, tiled=True)  8.45 us
    dot_general x1, matrix products, body(): jnp.dot(lax.all_gather(source, SEQ, axis=0, tiled=True), head, preferred_...  7.11 us
    all_to_all x1, starting transfers between devices, sent_and_summed(): lax.all_to_all(pieces, axis, split_axis=0, concat_axis=0, tiled=True)  7.02 us
    dot_general x1, matrix products, body(): lax.dot_general(score_grad, head, (((1,), (1,)), ((), ())), preferred_ele...  5.64 us
    all_to_all x1, starting transfers between devices, from_everyone(): lax.all_to_all(jnp.broadcast_to(array[None], (devices, *array.shape)), ax...  5.56 us
  transfers between devices with their start and end apart: 4, of which 3 were waited for; matrix products, arithmetic and copies ran while one was open for 2% of the time, Pallas kernels for 0%

commit v1 on v0

v1 whole, which is shorter than its diff:
```python
import functools

import jax
import jax.numpy as jnp
from jax import lax
from jax.experimental import pallas as pl
from jax.experimental.pallas import tpu as pltpu
from jax.sharding import Mesh
from jax.sharding import PartitionSpec as P

MESH = pl.DeviceIdType.MESH
ACT = 16
Y, X, CORE, Z = "seq_0", "seq_1", "seq_2", "vocab"
SEQ = (Y, X, CORE)
SIDE = 4
F32 = jnp.float32
BF16 = jnp.bfloat16
N_SEMS = 192


def block_row(half, p, q):
    return ((q * SIDE + p) if half == 0 else (p * SIDE + q)) * ACT


def kernel(
    mask_ref, hidden_hbm, head_hbm, pos_ref, avg_ref, grad_ref,
    raw, gathered, head, logits, part, near_half, near_full, far_half, far_full, total_own, total_in, final,
    table, moved, stat_x, stat_y, stat_z, pair, local_sem, send_sem, recv_sem,
):
    y, x, core, z = (lax.axis_index(a) for a in (Y, X, CORE, Z))
    depth = 8
    tokens, width = raw.shape
    vocab_here = head.shape[2]
    cut = width // 2
    quarter = cut // 2
    slice_z = width // depth
    blocks = SIDE * SIDE
    rows_all = blocks * ACT

    def ring(axis, at, size, step):
        return {axis: lax.rem(at + (step + size), size)}

    other = {CORE: 1 - core}
    peers = [other]
    peers += [ring(X, x, SIDE, k) for k in (1, 2, 3)]
    peers += [ring(Y, y, SIDE, k) for k in (1, 2, 3)]
    peers += [ring(Z, z, depth, k) for k in range(1, depth)]

    load_hidden = pltpu.make_async_copy(hidden_hbm, raw, local_sem.at[0])
    load_hidden.start()
    load_head = pltpu.make_async_copy(head_hbm, head.at[0], local_sem.at[1])
    load_head.start()
    barrier = pltpu.get_barrier_semaphore()
    for peer in peers:
        pl.semaphore_signal(barrier, inc=1, device_id=peer, device_id_type=MESH)

    mask = mask_ref[...]
    mask_f = jnp.broadcast_to(mask.astype(F32), (8, tokens)).astype(BF16)
    before = lax.broadcasted_iota(jnp.int32, (tokens, tokens), 0)
    after = lax.broadcasted_iota(jnp.int32, (tokens, tokens), 1)
    upper = jnp.where(before <= after, 1.0, 0.0).astype(BF16)
    count = jnp.dot(mask_f, upper, preferred_element_type=F32)[0:1, :]
    slot = lax.broadcasted_iota(jnp.int32, (ACT, tokens), 0).astype(F32) + 1.0
    chosen = (jnp.broadcast_to(count, (ACT, tokens)) == slot) & (
        jnp.broadcast_to(mask, (ACT, tokens)) == 1
    )
    picker_f = jnp.where(chosen, 1.0, 0.0).astype(F32)
    picker = picker_f.astype(BF16)
    valid = jnp.sum(picker_f, axis=1, keepdims=True)

    load_hidden.wait()
    for c in range(0, width, 1024):
        gathered[0:ACT, c : c + 1024] = jnp.dot(
            picker, raw[:, c : c + 1024], preferred_element_type=F32
        ).astype(BF16)

    pl.semaphore_wait(barrier, len(peers))
    sent, number = [], [0]

    def send(source, target, device):
        k = number[0]
        number[0] += 1
        copy = pltpu.make_async_remote_copy(
            src_ref=source, dst_ref=target, send_sem=send_sem.at[k], recv_sem=recv_sem.at[k],
            device_id=device, device_id_type=MESH,
        )
        copy.start()
        sent.append(copy)
        return copy

    axes = ((X, x), (Y, y))

    def near(half, step):
        axis, at = axes[half]
        return ring(axis, at, SIDE, step)

    def far(half, step):
        axis, at = axes[1 - half]
        return ring(axis, at, SIDE, step)

    def piece(ref, half, p, q, low, high):
        r = block_row(half, p, q)
        return ref.at[r : r + ACT, half * cut + low : half * cut + high]

    got = {}

    def send_far(half, p):
        whole = piece(gathered, half, p, 0, 0, cut)
        got[half, p, 3] = send(whole, piece(gathered, half, p, 3, 0, cut), far(half, 1))
        got[half, p, 1] = send(whole, piece(gathered, half, p, 1, 0, cut), far(half, -1))

    for half in (0, 1):
        whole = piece(gathered, half, 0, 0, 0, cut)
        got[half, 3, 0] = send(whole, piece(gathered, half, 3, 0, 0, cut), near(half, 1))
        got[half, 1, 0] = send(whole, piece(gathered, half, 1, 0, 0, cut), near(half, -1))
    swap = send(head_hbm, head.at[1], other)
    for half in (0, 1):
        send_far(half, 0)
    for half in (0, 1):
        got[half, 3, 0].wait_recv()
        low = piece(gathered, half, 3, 0, 0, quarter), piece(gathered, half, 2, 0, 0, quarter)
        got[half, 2, 0, 0] = send(*low, near(half, 1))
        got[half, 1, 0].wait_recv()
        high = piece(gathered, half, 1, 0, quarter, cut), piece(gathered, half, 2, 0, quarter, cut)
        got[half, 2, 0, 1] = send(*high, near(half, -1))
    for p in (3, 1):
        for half in (0, 1):
            send_far(half, p)

    def forward(half, p):
        got[half, p, 3].wait_recv()
        low = piece(gathered, half, p, 3, 0, quarter), piece(gathered, half, p, 2, 0, quarter)
        got[half, p, 2, 0] = send(*low, far(half, 1))
        got[half, p, 1].wait_recv()
        high = piece(gathered, half, p, 1, quarter, cut), piece(gathered, half, p, 2, quarter, cut)
        got[half, p, 2, 1] = send(*high, far(half, -1))

    for half in (0, 1):
        forward(half, 0)
    for half in (0, 1):
        got[half, 2, 0, 0].wait_recv()
        got[half, 2, 0, 1].wait_recv()
        send_far(half, 2)
    for p in (3, 1, 2):
        for half in (0, 1):
            forward(half, p)
    for p in range(SIDE):
        for half in (0, 1):
            got[half, p, 2, 0].wait_recv()
            got[half, p, 2, 1].wait_recv()

    load_head.wait()
    swap.wait_recv()
    step_k = 1024
    for j in (0, 1):
        columns = slice(j * vocab_here, (j + 1) * vocab_here)
        logits[:, columns] = jnp.dot(
            gathered[:, 0:step_k], head[j, 0:step_k, :], preferred_element_type=F32
        )

        @pl.loop(1, width // step_k)
        def _(k):
            at = pl.ds(pl.multiple_of(k * step_k, step_k), step_k)
            logits[:, columns] += jnp.dot(
                gathered[:, at], head[j, at, :], preferred_element_type=F32
            )

    local = logits[...]
    top = jnp.max(local, axis=1, keepdims=True)
    ex = jnp.exp(local - top)
    sum_ex = jnp.sum(ex, axis=1, keepdims=True)
    sum_weighted = jnp.sum(ex * local, axis=1, keepdims=True)
    lane = lax.broadcasted_iota(jnp.int32, (rows_all, 128), 1)
    flags = jnp.concatenate([valid, jnp.zeros((rows_all - ACT, 1), F32)], axis=0)
    columns_in = jnp.where(
        lane == 0, top, jnp.where(lane == 1, sum_ex, jnp.where(lane == 2, sum_weighted, flags))
    )

    def absolute(r):
        dy, dx = divmod(r, SIDE)
        place = lax.rem(y + dy, SIDE) * SIDE + lax.rem(x + dx, SIDE)
        return pl.ds(pl.multiple_of(place * ACT, ACT), ACT)

    for r in range(blocks):
        table[absolute(r), :] = columns_in[r * ACT : (r + 1) * ACT, :]
    mine = table[...].T[0:8, :]

    def exchange(own, slots, axis, at, size):
        slots[at] = own
        for k in range(1, size):
            base = number[0]
            number[0] += 1
            pltpu.make_async_remote_copy(
                src_ref=slots.at[at], dst_ref=slots.at[at], send_sem=send_sem.at[base], recv_sem=recv_sem.at[base],
                device_id=ring(axis, at, size, k), device_id_type=MESH,
            ).start()
            came = lax.rem(at + (size - k), size)
            sent.append(
                pltpu.make_async_remote_copy(
                    src_ref=slots.at[at], dst_ref=slots.at[came], send_sem=send_sem.at[base], recv_sem=recv_sem.at[base],
                    device_id=ring(axis, at, size, k), device_id_type=MESH,
                )
            )
        for copy in sent[len(sent) - (size - 1) :]:
            copy.wait_recv()
        tops = [slots[k][0:1, :] for k in range(size)]
        best = functools.reduce(jnp.maximum, tops)
        scales = [jnp.exp(t - best) for t in tops]
        sums = sum(slots[k][1:2, :] * scales[k] for k in range(size))
        weights = sum(slots[k][2:3, :] * scales[k] for k in range(size))
        marks = functools.reduce(jnp.maximum, [slots[k][3:4, :] for k in range(size)])
        return jnp.concatenate([best, sums, weights, marks, jnp.zeros((4, best.shape[1]), F32)], axis=0)

    mine = exchange(mine, stat_x, X, x, SIDE)
    mine = exchange(mine, stat_y, Y, y, SIDE)
    mine = exchange(mine, stat_z, Z, z, depth)
    best, sums, weights, marks = (mine[k : k + 1, :] for k in range(4))
    mean = weights / sums
    entropy = best + jnp.log(sums) - mean
    summed = jnp.sum(entropy * marks, axis=1, keepdims=True)
    counted = jnp.sum(marks, axis=1, keepdims=True)
    row8 = lax.broadcasted_iota(jnp.int32, (8, 128), 0)
    pair[core] = jnp.where(row8 == 0, summed, counted)
    k_pair = number[0]
    number[0] += 1
    pltpu.make_async_remote_copy(
        src_ref=pair.at[core], dst_ref=pair.at[core], send_sem=send_sem.at[k_pair], recv_sem=recv_sem.at[k_pair],
        device_id=other, device_id_type=MESH,
    ).start()
    pair_in = pltpu.make_async_remote_copy(
        src_ref=pair.at[core], dst_ref=pair.at[1 - core], send_sem=send_sem.at[k_pair], recv_sem=recv_sem.at[k_pair],
        device_id=other, device_id_type=MESH,
    )
    sent.append(pair_in)

    back = jnp.concatenate([best, sums, mean, entropy, jnp.zeros((124, rows_all), F32)], axis=0)
    table[...] = back.T
    for r in range(blocks):
        moved[r * ACT : (r + 1) * ACT, :] = table[absolute(r), :]
    row_top, row_sum, row_mean = (moved[:, k : k + 1] for k in range(3))
    value = logits[...]
    score = (-((jnp.exp(value - row_top) / row_sum) * (value - row_mean))).astype(BF16)
    scores = [score[:, 0:vocab_here], score[:, vocab_here : 2 * vocab_here]]

    step_d = 512

    @pl.loop(0, width // step_d)
    def _(k):
        at = pl.ds(pl.multiple_of(k * step_d, step_d), step_d)
        both = [
            lax.dot_general(scores[j], head[j, at, :], (((1,), (1,)), ((), ())), preferred_element_type=F32)
            for j in (0, 1)
        ]
        part[:, at] = (both[0] + both[1]).astype(BF16)

    def add_into(target, source):
        target[...] = (target[...].astype(F32) + source[...].astype(F32)).astype(BF16)

    order = (2, 1, 3, 0)
    half_in, full_in, near_in = {}, {}, {}
    for p in order:
        for half in (0, 1):
            half_in[half, p, 1] = send(
                piece(part, half, p, 2, 0, quarter), far_half.at[half, p, 0], far(half, 1)
            )
            half_in[half, p, 3] = send(
                piece(part, half, p, 2, quarter, cut), far_half.at[half, p, 1], far(half, -1)
            )
    for p in order:
        for half in (0, 1):
            half_in[half, p, 1].wait_recv()
            add_into(piece(part, half, p, 1, 0, quarter), far_half.at[half, p, 0])
            full_in[half, p, 0] = send(piece(part, half, p, 1, 0, cut), far_full.at[half, p, 0], far(half, 1))
            half_in[half, p, 3].wait_recv()
            add_into(piece(part, half, p, 3, quarter, cut), far_half.at[half, p, 1])
            full_in[half, p, 1] = send(piece(part, half, p, 3, 0, cut), far_full.at[half, p, 1], far(half, -1))
    for p in order:
        for half in (0, 1):
            for side in (0, 1):
                full_in[half, p, side].wait_recv()
            mine_ref = piece(part, half, p, 0, 0, cut)
            ends = far_full[half, p, 0].astype(F32) + far_full[half, p, 1].astype(F32)
            mine_ref[...] = (mine_ref[...].astype(F32) + ends).astype(BF16)
            if p == 2:
                near_in[half, 1] = send(piece(part, half, 2, 0, 0, quarter), near_half.at[half, 0], near(half, 1))
                near_in[half, 3] = send(piece(part, half, 2, 0, quarter, cut), near_half.at[half, 1], near(half, -1))
            if p == 1:
                near_in[half, 1].wait_recv()
                add_into(piece(part, half, 1, 0, 0, quarter), near_half.at[half, 0])
                near_in[half, 0, 0] = send(piece(part, half, 1, 0, 0, cut), near_full.at[half, 0], near(half, 1))
            if p == 3:
                near_in[half, 3].wait_recv()
                add_into(piece(part, half, 3, 0, quarter, cut), near_half.at[half, 1])
                near_in[half, 0, 1] = send(piece(part, half, 3, 0, 0, cut), near_full.at[half, 1], near(half, -1))
    for half in (0, 1):
        near_in[half, 0, 0].wait_recv()
        near_in[half, 0, 1].wait_recv()
        ends = near_full[half, 0].astype(F32) + near_full[half, 1].astype(F32)
        own = (piece(part, half, 0, 0, 0, cut)[...].astype(F32) + ends).astype(BF16)
        for k in range(depth // 2):
            total_own[half * (depth // 2) + k] = own[:, k * slice_z : (k + 1) * slice_z]

    arrivals = []
    for k in range(1, depth):
        s = number[0]
        number[0] += 1
        target = lax.rem(z + k, depth)
        copy = pltpu.make_async_remote_copy(
            src_ref=total_own.at[target], dst_ref=total_in.at[k - 1], send_sem=send_sem.at[s], recv_sem=recv_sem.at[s],
            device_id={Z: target}, device_id_type=MESH,
        )
        copy.start()
        sent.append(copy)
        arrivals.append(copy)

    pair_in.wait_recv()
    sums_of = pair[0] + pair[1]
    avg_ref[...] = sums_of[0:1, :] / sums_of[1:2, :]
    pos_ref[...] = jnp.sum(picker_f * moved[0:ACT, 3:4], axis=0, keepdims=True)
    spread = picker_f.T.astype(BF16)

    gradient = total_own[z].astype(F32)
    for k, copy in enumerate(arrivals):
        copy.wait_recv()
        gradient = gradient + total_in[k].astype(F32)
    grad_ref[...] = jnp.dot(spread, gradient.astype(BF16), preferred_element_type=F32).astype(BF16)
    for copy in sent:
        copy.wait_send()


def body(hidden, head, mask):
    tokens, width = hidden.shape
    vocab_here = head.shape[1]
    depth = lax.axis_size(Z)
    blocks = SIDE * SIDE
    cut = width // 2
    quarter = cut // 2
    vmem = functools.partial(pl.BlockSpec, memory_space=pltpu.VMEM)
    hbm = functools.partial(pl.BlockSpec, memory_space=pl.ANY)
    pos, avg, grad = pl.pallas_call(
        kernel,
        out_shape=(
            jax.ShapeDtypeStruct((1, tokens), F32),
            jax.ShapeDtypeStruct((1, 128), F32),
            jax.ShapeDtypeStruct((tokens, width // depth), BF16),
        ),
        in_specs=[vmem(), hbm(), hbm()],
        out_specs=(vmem(), vmem(), vmem()),
        scratch_shapes=[
            pltpu.VMEM((tokens, width), BF16),
            pltpu.VMEM((blocks * ACT, width), BF16),
            pltpu.VMEM((2, width, vocab_here), BF16),
            pltpu.VMEM((blocks * ACT, 2 * vocab_here), F32),
            pltpu.VMEM((blocks * ACT, width), BF16),
            pltpu.VMEM((2, 2, ACT, quarter), BF16),
            pltpu.VMEM((2, 2, ACT, cut), BF16),
            pltpu.VMEM((2, SIDE, 2, ACT, quarter), BF16),
            pltpu.VMEM((2, SIDE, 2, ACT, cut), BF16),
            pltpu.VMEM((depth, ACT, width // depth), BF16),
            pltpu.VMEM((depth - 1, ACT, width // depth), BF16),
            pltpu.VMEM((ACT, width // depth), F32),
            pltpu.VMEM((blocks * ACT, 128), F32),
            pltpu.VMEM((blocks * ACT, 128), F32),
            pltpu.VMEM((SIDE, 8, blocks * ACT), F32),
            pltpu.VMEM((SIDE, 8, blocks * ACT), F32),
            pltpu.VMEM((depth, 8, blocks * ACT), F32),
            pltpu.VMEM((2, 8, 128), F32),
            pltpu.SemaphoreType.DMA((2,)),
            pltpu.SemaphoreType.DMA((N_SEMS,)),
            pltpu.SemaphoreType.DMA((N_SEMS,)),
        ],
        compiler_params=pltpu.CompilerParams(
            collective_id=0, has_side_effects=True, vmem_limit_bytes=60 * 2**20
        ),
        name="entropy_bonus",
    )(mask.reshape(1, tokens), hidden, head)
    return pos.reshape(tokens), avg[0, 0], grad


def solution(mesh):
    finer = Mesh(mesh.devices.reshape(SIDE, SIDE, 2, mesh.shape["vocab"]), (Y, X, CORE, Z))
    return jax.shard_map(
        body,
        mesh=finer,
        in_specs=(P(SEQ, None), P(None, (*SEQ, Z)), P(SEQ)),
        out_specs=(P(SEQ), P(), P(SEQ, Z)),
        check_vma=False,
    )
```

time: 264 us -> 95.2 us (0.36)
  waiting for transfers between devices: 158 us -> 0 us
  Pallas kernels: 0 us -> 90 us
  blocking collectives: 51.7 us -> 0 us
  matrix products: 16.3 us -> 0 us
  between operations: 16.7 us -> 2.32 us
  starting transfers between devices: 12.7 us -> 0 us
  other arithmetic: 3.53 us -> 0 us
    pallas_call x0 -> x1, Pallas kernels: none -> 90 us  [body(): pl.pallas_call(kernel, out_shape=(jax.ShapeDtypeStruct((1, tokens), F32),...]
    reduce_scatter x1 -> x0, waiting for transfers between devices: 88.1 us -> none  [body(): lax.psum_scatter(lax.dot_general(score_grad, head, (((1,), (1,)), ((), ()...]
    all_gather x1 -> x0, waiting for transfers between devices: 61.6 us -> none  [body(): lax.all_gather(source, SEQ, axis=0, tiled=True)]
    all_gather x4 -> x0, blocking collectives: 51.7 us -> none  [gathered_once(): both, at, found = (lax.all_gather(jnp.concatenate(lines), axis), 0, {})]
    dot_general x5 -> x0, matrix products: 16.3 us -> none  [the longest x1 7.11 us: body(): jnp.dot(lax.all_gather(source, SEQ, axis=0, tiled=True), head, preferred_...]
    all_to_all x2 -> x0, starting transfers between devices: 12.6 us -> none  [the longest x1 7.02 us: sent_and_summed(): lax.all_to_all(pieces, axis, split_axis=0, concat_axis=0, tiled=True)]
    all_to_all x2 -> x0, waiting for transfers between devices: 8.45 us -> none  [the longest x1 8.45 us: sent_and_summed(): lax.all_to_all(pieces, axis, split_axis=0, concat_axis=0, tiled=True)]
  transfers between devices with their start and end apart: 4 -> 0, of which waited for: 3 -> 0; matrix products, arithmetic and copies ran while one was open for 2% -> 0% of each run, Pallas kernels for 0% -> 0%
where the time goes in v1:
time: 95.2 us; the launch traced here: 95.1 us
  Pallas kernels  90 us (95%)
  local copies, waits for them, and re-layouts  2.8 us (3%)
  between operations  2.32 us (2%)
    pallas_call x1, Pallas kernels, body(): pl.pallas_call(kernel, out_shape=(jax.ShapeDtypeStruct((1, tokens), F32),...  90 us
    unnamed x2, local copies, waits for them, and re-layouts  2.8 us

profile of v1, /device:TPU:2, one launch (start us, length us, event | category | flops | bytes accessed | tf_op | source)
XLA Modules:
  0.0 95.1 jit_solution(1755154560063494443)
XLA Ops:
  0.6 90.0 %entropy_bonus.1 = (f32[1,128]{1,0:T(1,128)}, f32[1,128]{1,0:T(1,128)}, bf16[128,1024]{1,0:T(8,128)(2,1)}) custom-call(s32[1,128]{1,0:T(1,128)} %bitcast.4, bf16[128,8192]{1,0:T(8,128)(2,1)} %hidden_hbm.1, bf16[8192,256]{1,0:T(8,128)(2,1)} %head_hbm.1), custom_call_target="tpu_custom_call" | custom-call | tf_op jit(solution)/shard_map/entropy_bonus/pallas_call | solution.py:340
  90.6 1.1 %copy.9 = f32[128]{0:T(128)} copy(f32[128]{0:T(128)} %bitcast.6) | data formatting | bytes 1024
  92.3 1.7 %copy.11 = bf16[128,1024]{1,0:T(8,128)(2,1)} copy(bf16[128,1024]{1,0:T(8,128)(2,1)} %get-tuple-element.14) | data formatting | bytes 524288
